TPU v7x, 256 devices: a whole 4x4x8 slice. The times are simulated.
256 devices in a mesh: section: 8 (over z), ex: 4 (over x), ey: 8 (over y, core).
Axes of the slice: x: 4, y: 4, z: 8, core: 2. Of those that a mesh axis runs over, the one named last changes fastest.
Arguments:
- section_out: bfloat16 [8, 2048, 7168], P('section', ('ex', 'ey')), may hold values from -6 to 6
- expert_ids: int32 [8, 2048, 2], P('section', ('ex', 'ey')), may hold values from 0 to 7, all different within a row; in each aligned block of 64 rows (0 to 63, 64 to 127, ..., all dimensions but the last counted through in order) at most 24 rows name the same one
- gate_weights: float32 [8, 2048, 2], P('section', ('ex', 'ey')), may hold values from 0.1 to 1
- w_gate_up: bfloat16 [8, 8, 7168, 2, 1024], P('section', 'ey', None, None, 'ex'), may hold values from -0.0625 to 0.0625
- w_down: bfloat16 [8, 8, 1024, 7168], P('section', 'ey', 'ex'), may hold values from -0.1875 to 0.1875
Outputs:
- next_state: bfloat16 [8, 2048, 7168], P('section', ('ex', 'ey'))
Inputs may be any that keep to these rules, and one draw needn't show every extreme that they name: `expert_ids`: each row names 2 different experts. In the rows of one device (aligned blocks of 64 rows, all leading dimensions in order) no expert is named by more than 24 rows, and some block of every draw names one expert exactly 24 times.
All inputs are finite; a program needn't handle non-finite values.
Results may differ from a plain program's by a relative error of at most 0.008.
Values may be sent and summed in bfloat16 or wider, within the bound.
A program may use at most 128 MiB of HBM per device.

v0:
```python
import jax
import jax.numpy as jnp
from jax import lax
from jax.sharding import PartitionSpec as P


def shifted(value, axis, steps):
    count = lax.axis_size(axis)
    pairs = [(source, (source + steps) % count) for source in range(count)]
    return lax.ppermute(value, axis, pairs)


def expert_hidden(token_rows, gate_up, unit_count):
    mixed = jnp.dot(token_rows, gate_up, preferred_element_type=jnp.float32)
    return (jax.nn.silu(mixed[:, :unit_count]) * mixed[:, unit_count:]).astype(jnp.bfloat16)


def on_device(section_out, expert_ids, gate_weights, w_gate_up, w_down):
    tok_rows = section_out.shape[1]
    model_width = section_out.shape[2]
    top_count = expert_ids.shape[2]
    experts = lax.axis_size("ey")
    capacity = min(tok_rows, 3 * tok_rows * top_count // (2 * experts))
    unit_count = w_down.shape[2]
    gate_up = w_gate_up[0, 0].reshape(model_width, 2 * unit_count)
    down_rows = w_down[0, 0]
    incoming = shifted(section_out, "section", 1)[0]
    chosen = expert_ids[0].reshape(-1)
    one_hot = (chosen[:, None] == jnp.arange(experts, dtype=jnp.int32)[None, :]).astype(jnp.int32)
    slot_rank = jnp.sum((jnp.cumsum(one_hot, axis=0) - one_hot) * one_hot, axis=1)
    position = chosen * capacity + slot_rank
    token_of = jnp.arange(tok_rows * top_count, dtype=jnp.int32) // top_count
    filled = jnp.zeros((experts * capacity,), jnp.int32).at[position].set(1)
    source_row = jnp.zeros((experts * capacity,), jnp.int32).at[position].set(token_of)
    outgoing = jnp.where(filled[:, None] > 0, incoming[source_row], jnp.zeros((), jnp.bfloat16))
    arrived = lax.all_to_all(
        outgoing.reshape(experts, capacity, model_width),
        "ey",
        split_axis=0,
        concat_axis=0,
        tiled=True,
    ).reshape(experts * capacity, model_width)
    hidden_all = expert_hidden(
        lax.all_gather(arrived, "ex", axis=0, tiled=True), gate_up, unit_count
    )
    summed = lax.psum_scatter(
        jnp.dot(hidden_all, down_rows, preferred_element_type=jnp.float32).astype(jnp.bfloat16),
        "ex",
        scatter_dimension=0,
        tiled=True,
    )
    expert_out = lax.all_to_all(
        summed.reshape(experts, capacity, model_width),
        "ey",
        split_axis=0,
        concat_axis=0,
        tiled=True,
    ).reshape(experts * capacity, model_width)
    picked = expert_out[position].reshape(tok_rows, top_count, model_width)
    weighted = jnp.einsum("tkd,tk->td", picked.astype(jnp.float32), gate_weights[0])
    result = (incoming.astype(jnp.float32) + weighted).astype(jnp.bfloat16)
    return result[None]


def solution(mesh):
    return jax.shard_map(
        on_device,
        mesh=mesh,
        in_specs=(
            P("section", ("ex", "ey"), None),
            P("section", ("ex", "ey"), None),
            P("section", ("ex", "ey"), None),
            P("section", "ey", None, None, "ex"),
            P("section", "ey", "ex", None),
        ),
        out_specs=P("section", ("ex", "ey"), None),
        check_vma=False,
    )
```

profile of v0, /device:TPU:1, one launch (start us, length us, event | category | flops | bytes accessed | tf_op | source)
XLA Modules:
  0.0 363.6 jit_solution(1292893236069667634)
XLA Ops:
  6.5 2.5 collective-permute-start
  9.0 0.8 copy.9
  9.8 0.7 broadcast_multiply_fusion
  10.4 0.1 eq.15
  10.6 0.1 fusion.6
  10.7 0.1 copy.8
  10.8 0.1 mul.28
  10.9 0.2 reduce_window_sum.11
  11.1 0.2 select_reduce_fusion
  11.3 1.0 scatter_custom_fusion.1
  12.3 1.0 scatter_custom_fusion
  13.3 0.1 broadcast_in_dim.29
  13.4 19.8 %collective-permute-done = bf16[1,64,7168]{2,1,0:T(8,128)(2,1)S(1)} collective-permute-done((bf16[1,64,7168]{2,1,0:T(8,128)(2,1)}, bf16[1,64,7168]{2,1,0:T(8,128)(2,1)S(1)}, u32[]{:S(2)}, u32[]{:S(2)}) %collective-permute-start) | collective-permute-done | bytes 917536 | tf_op jit(solution)/shard_map/ppermute | solution.py:10
  33.2 3.8 %gather_fusion = bf16[192,7168]{1,0:T(8,128)(2,1)} fusion(bf16[64,7168]{1,0:T(8,128)(2,1)S(1)} %bitcast.32, s32[1024]{0:T(1024)S(1)} %pad_clamp_fusion.1), kind=kCustom, calls=%fused_computation | custom fusion | bytes 5505792 | tf_op jit(solution)/shard_map/gather | solution.py:35
  37.0 2.0 broadcast_select_fusion
  39.1 39.0 %all_to_all.10 = bf16[8,24,7168]{2,1,0:T(8,128)(2,1)} all-to-all(bf16[8,24,7168]{2,1,0:T(8,128)(2,1)S(1)} %broadcast_select_fusion), channel_id=1, replica_groups=mesh['section'=8,'ex'=4,'ey'=8] {'ey'}, dimensions={0} | all-to-all | bytes 5505024 | tf_op jit(solution)/shard_map/all_to_all | solution.py:36
  78.1 0.0 all-gather.2.cloned.1.call-update
  78.1 0.0 reduce-scatter.2.cloned.1.call-start
  78.1 7.4 %copy.12 = bf16[896,8,2,256]{3,1,2,0:T(8,128)(2,1)} copy(bf16[896,8,2,256]{3,2,1,0:T(2,128)(2,1)} %bitcast.35) | data formatting | bytes 14680064
  85.5 98.6 %all-gather.2.cloned.1.call-done = bf16[768,7168]{1,0:T(8,128)(2,1)} async-done(((bf16[192,7168]{1,0:T(8,128)(2,1)}), bf16[768,7168]{1,0:T(8,128)(2,1)}) %all-gather.2.cloned.1.call-update) | async-done | bytes 11010064 | tf_op jit(solution)/shard_map/all_gather | solution.py:44
  184.1 10.9 %fusion.13 = f32[768,512]{1,0:T(8,128)S(1)} fusion(bf16[768,7168]{1,0:T(8,128)(2,1)} %all-gather.2.cloned.1.call-done, bf16[7168,512]{1,0:T(8,128)(2,1)} %bitcast.36), kind=kOutput, calls=%fused_computation.33 | convolution fusion | flops 5637144576 | bytes 19922944 | tf_op jit(solution)/shard_map/dot_general | solution.py:14
  195.0 5.8 %convolution_convert_fusion = bf16[768,7168]{1,0:T(8,128)(2,1)} fusion(bf16[1,1,256,7168]{3,2,1,0:T(8,128)(2,1)S(1)} %copy-done, f32[768,512]{1,0:T(8,128)S(1)} %fusion.13), kind=kOutput, calls=%fused_computation.4 | convolution fusion | flops 2825256960 | bytes 16252928 | tf_op jit(solution)/shard_map/dot_general | solution.py:47
  200.7 0.0 reduce-scatter.2.cloned.1.call-update
  200.8 105.6 %reduce-scatter.2.cloned.1.call-done = bf16[192,7168]{1,0:T(8,128)(2,1)} async-done(((bf16[768,7168]{1,0:T(8,128)(2,1)}), bf16[192,7168]{1,0:T(8,128)(2,1)}) %reduce-scatter.2.cloned.1.call-update) | async-done | bytes 2752528 | tf_op jit(solution)/shard_map/reduce_scatter | solution.py:46
  306.3 5.1 %all-to-all-start.1 = ((bf16[8,24,7168]{2,1,0:T(8,128)(2,1)}), bf16[8,24,7168]{2,1,0:T(8,128)(2,1)}, u32[]{:S(2)}, u32[]{:S(2)}) async-start(bf16[8,24,7168]{2,1,0:T(8,128)(2,1)} %bitcast.37), calls=%async_computation.2 | async-start | bytes 5505024 | tf_op jit(solution)/shard_map/all_to_all | solution.py:52
  311.5 0.0 copy-done.1
  311.5 0.1 copy.10
  311.6 33.2 %all-to-all-done.1 = bf16[8,24,7168]{2,1,0:T(8,128)(2,1)} async-done(((bf16[8,24,7168]{2,1,0:T(8,128)(2,1)}), bf16[8,24,7168]{2,1,0:T(8,128)(2,1)}, u32[]{:S(2)}, u32[]{:S(2)}) %all-to-all-start.1) | async-done | bytes 2752544 | tf_op jit(solution)/shard_map/all_to_all | solution.py:52
  344.8 5.5 %gather_fusion.1 = bf16[128,7168]{1,0:T(8,128)(2,1)S(1)} fusion(bf16[192,7168]{1,0:T(8,128)(2,1)} %bitcast.7, s32[1024]{0:T(1024)S(1)} %pad_clamp_fusion), kind=kCustom, calls=%fused_computation.1 | custom fusion | bytes 3670528 | tf_op jit(solution)/shard_map/gather | solution.py:59
  350.3 1.7 reshape.53
  352.0 3.5 fusion.14
  355.5 1.3 fusion.2
  (11 shorter events, 0.0 us)
Async XLA Ops:
  6.5 177.5 %all-gather.2.cloned.1.call-start = ((), (), s32[]{:S(2)}) async-start(), calls=%async_computation.3 | async-start | bytes 13762560 | tf_op jit(solution)/shard_map/all_gather | solution.py:44
  6.5 26.7 %collective-permute-start = (bf16[1,64,7168]{2,1,0:T(8,128)(2,1)}, bf16[1,64,7168]{2,1,0:T(8,128)(2,1)S(1)}, u32[]{:S(2)}, u32[]{:S(2)}) collective-permute-start(bf16[1,64,7168]{2,1,0:T(8,128)(2,1)} %param.5), channel_id=1, source_target_pairs={{0,32},{32,64},{64,96},{96,128},{128,160},{160,192},{192,224},{224... | collective-permute-start | bytes 2752520 | tf_op jit(solution)/shard_map/ppermute | solution.py:10
  78.1 228.2 %reduce-scatter.2.cloned.1.call-start = ((), (), s32[]{:S(2)}) async-start(), calls=%async_computation.4 | async-start | bytes 13762560 | tf_op jit(solution)/shard_map/reduce_scatter | solution.py:46
  184.1 10.9 %copy-start = (bf16[1,1,256,7168]{3,2,1,0:T(8,128)(2,1)S(1)}, bf16[1,1,256,7168]{3,2,1,0:T(8,128)(2,1)}, u32[]{:S(2)}) copy-start(bf16[1,1,256,7168]{3,2,1,0:T(8,128)(2,1)} %param.9) | copy-start | bytes 11010052
  306.3 5.2 %copy-start.1 = (f32[1,64,2]{1,2,0:T(2,128)S(1)}, f32[1,64,2]{1,2,0:T(2,128)}, u32[]{:S(2)}) copy-start(f32[1,64,2]{1,2,0:T(2,128)} %param.7) | copy-start | bytes 1540
  306.3 38.5 %all-to-all-start.1 = ((bf16[8,24,7168]{2,1,0:T(8,128)(2,1)}), bf16[8,24,7168]{2,1,0:T(8,128)(2,1)}, u32[]{:S(2)}, u32[]{:S(2)}) async-start(bf16[8,24,7168]{2,1,0:T(8,128)(2,1)} %bitcast.37), calls=%async_computation.2 | async-start | bytes 5505024 | tf_op jit(solution)/shard_map/all_to_all | solution.py:52
Sparse Core Ops, SparseCore 0:
  78.2 105.8 all-gather.1
  200.9 105.3 reduce-scatter.1
where the time goes:
time: 364 us
  waiting for transfers between devices  257 us (71%)
  blocking collectives  39 us (11%)
  local copies, waits for them, and re-layouts  21.7 us (6%)
  matrix products  20.2 us (6%)
  between operations  13.5 us (4%)
  starting transfers between devices  7.65 us (2%)
  other arithmetic  4.43 us (1%)
    reduce_scatter x1, waiting for transfers between devices, on_device(): lax.psum_scatter(jnp.dot(hidden_all, down_rows, preferred_element_type=jn...  106 us
    all_gather x1, waiting for transfers between devices, on_device(): lax.all_gather(arrived, 'ex', axis=0, tiled=True)  98.6 us
    all_to_all x1, blocking collectives, on_device(): lax.all_to_all(outgoing.reshape(experts, capacity, model_width), 'ey', sp...  39 us
    all_to_all x1, waiting for transfers between devices, on_device(): lax.all_to_all(summed.reshape(experts, capacity, model_width), 'ey', spli...  33.2 us
    ppermute x1, waiting for transfers between devices, shifted(): return lax.ppermute(value, axis, pairs)  19.8 us
    dot_general x1, matrix products, expert_hidden(): mixed = jnp.dot(token_rows, gate_up, preferred_element_type=jnp.float32)  10.9 us
    unnamed x6, local copies, waits for them, and re-layouts  8.14 us
  transfers between devices with their start and end apart: 4, of which 4 were waited for; matrix products, arithmetic and copies ran while one was open for 3% of the time, Pallas kernels for 0%

commit v1 on v0

--- a/solution.py
+++ b/solution.py
@@ -2,6 +2,27 @@
 import jax.numpy as jnp
 from jax import lax
 from jax.sharding import PartitionSpec as P
+
+
+def ring_gather(array, axis, dim):
+    size, index, rows = (lax.axis_size(axis), lax.axis_index(axis), array.shape[dim])
+    upward = [(i, (i + 1) % size) for i in range(size)]
+    left = [(i, (i - 1) % size) for i in range(size)]
+    result = jnp.zeros((*array.shape[:dim], size * rows, *array.shape[dim + 1 :]), array.dtype)
+    result = lax.dynamic_update_slice_in_dim(result, array, index * rows, axis=dim)
+    from_left = from_right = array
+    half = size // 2
+    for step in range(1, half + 1):
+        from_left = lax.ppermute(from_left, axis, upward)
+        result = lax.dynamic_update_slice_in_dim(
+            result, from_left, (index - step) % size * rows, axis=dim
+        )
+        if step < size - half:
+            from_right = lax.ppermute(from_right, axis, left)
+            result = lax.dynamic_update_slice_in_dim(
+                result, from_right, (index + step) % size * rows, axis=dim
+            )
+    return result
 
 
 def shifted(value, axis, steps):
@@ -40,9 +61,7 @@
         concat_axis=0,
         tiled=True,
     ).reshape(experts * capacity, model_width)
-    hidden_all = expert_hidden(
-        lax.all_gather(arrived, "ex", axis=0, tiled=True), gate_up, unit_count
-    )
+    hidden_all = expert_hidden(ring_gather(arrived, "ex", 0), gate_up, unit_count)
     summed = lax.psum_scatter(
         jnp.dot(hidden_all, down_rows, preferred_element_type=jnp.float32).astype(jnp.bfloat16),
         "ex",

time: 364 us -> 377 us (1.036)
  local copies, waits for them, and re-layouts: 21.7 us -> 31.7 us
    ppermute x0 -> x3, waiting for transfers between devices: none -> 105 us  [the longest x2 105 us: ring_gather(): from_left = lax.ppermute(from_left, axis, upward)]
    all_gather x1 -> x0, waiting for transfers between devices: 98.6 us -> none  [on_device(): lax.all_gather(arrived, 'ex', axis=0, tiled=True)]
    dynamic_update_slice x0 -> x4, local copies, waits for them, and re-layouts: none -> 8.73 us  [the longest x2 4.36 us: ring_gather(): lax.dynamic_update_slice_in_dim(result, from_left, (index - step) % size...]
    dot_general x1, matrix products: 10.9 us -> 6.96 us  [expert_hidden(): mixed = jnp.dot(token_rows, gate_up, preferred_element_type=jnp.float32)]
    unnamed x6 -> x10, local copies, waits for them, and re-layouts: 8.14 us -> 8.11 us
  transfers between devices with their start and end apart: 4 -> 6, of which waited for: 4 -> 5; matrix products, arithmetic and copies ran while one was open for 3% -> 5% of each run, Pallas kernels for 0% -> 0%
where the time goes in v1:
time: 377 us
  waiting for transfers between devices  260 us (69%)
  blocking collectives  39 us (10%)
  local copies, waits for them, and re-layouts  31.7 us (8%)
  matrix products  17.7 us (5%)
  between operations  13.6 us (4%)
  starting transfers between devices  10.3 us (3%)
  other arithmetic  4.43 us (1%)
    ppermute x2, waiting for transfers between devices, ring_gather(): from_left = lax.ppermute(from_left, axis, upward)  105 us
    reduce_scatter x1, waiting for transfers between devices, on_device(): lax.psum_scatter(jnp.dot(hidden_all, down_rows, preferred_element_type=jn...  102 us
    all_to_all x1, blocking collectives, on_device(): lax.all_to_all(outgoing.reshape(experts, capacity, model_width), 'ey', sp...  39 us
    all_to_all x1, waiting for transfers between devices, on_device(): lax.all_to_all(summed.reshape(experts, capacity, model_width), 'ey', spli...  33.2 us
    ppermute x1, waiting for transfers between devices, shifted(): return lax.ppermute(value, axis, pairs)  19.8 us
    unnamed x10, local copies, waits for them, and re-layouts  8.11 us
  transfers between devices with their start and end apart: 6, of which 5 were waited for; matrix products, arithmetic and copies ran while one was open for 5% of the time, Pallas kernels for 0%

profile of v1, /device:TPU:1, one launch (start us, length us, event | category | flops | bytes accessed | tf_op | source)
XLA Modules:
  0.0 376.8 jit_solution(10377472866339742364)
XLA Ops:
  6.5 2.5 collective-permute-start
  9.0 0.8 copy.9
  9.8 0.7 broadcast_multiply_fusion
  10.4 0.1 eq.19
  10.8 0.1 mul.40
  10.9 0.2 reduce_window_sum.11
  11.1 0.2 select_reduce_fusion
  11.3 1.0 scatter_custom_fusion.1
  12.3 1.0 scatter_custom_fusion
  13.4 19.8 %collective-permute-done = bf16[1,64,7168]{2,1,0:T(8,128)(2,1)S(1)} collective-permute-done((bf16[1,64,7168]{2,1,0:T(8,128)(2,1)}, bf16[1,64,7168]{2,1,0:T(8,128)(2,1)S(1)}, u32[]{:S(2)}, u32[]{:S(2)}) %collective-permute-start) | collective-permute-done | bytes 917536 | tf_op jit(solution)/shard_map/ppermute | solution.py:31
  33.2 3.9 %gather_fusion = bf16[192,7168]{1,0:T(8,128)(2,1)} fusion(bf16[64,7168]{1,0:T(8,128)(2,1)S(1)} %bitcast.32, s32[1024]{0:T(1024)S(1)} %pad_clamp_fusion.1), kind=kCustom, calls=%fused_computation | custom fusion | bytes 5505792 | tf_op jit(solution)/shard_map/gather | solution.py:56
  37.0 2.0 broadcast_select_fusion
  39.1 39.0 %all_to_all.10 = bf16[8,24,7168]{2,1,0:T(8,128)(2,1)} all-to-all(bf16[8,24,7168]{2,1,0:T(8,128)(2,1)S(1)} %broadcast_select_fusion), channel_id=1, replica_groups=mesh['section'=8,'ex'=4,'ey'=8] {'ey'}, dimensions={0} | all-to-all | bytes 5505024 | tf_op jit(solution)/shard_map/all_to_all | solution.py:57
  78.1 1.2 collective-permute-start.1
  79.3 1.5 collective-permute-start.2
  80.7 59.2 %collective-permute-done.1 = bf16[192,7168]{1,0:T(8,128)(2,1)} collective-permute-done((bf16[192,7168]{1,0:T(8,128)(2,1)}, bf16[192,7168]{1,0:T(8,128)(2,1)}, u32[]{:S(2)}, u32[]{:S(2)}) %collective-permute-start.1) | collective-permute-done | bytes 2752544 | tf_op jit(solution)/shard_map/ppermute | solution.py:16
  140.0 7.3 %copy.12 = bf16[896,8,2,256]{3,1,2,0:T(8,128)(2,1)} copy(bf16[896,8,2,256]{3,2,1,0:T(2,128)(2,1)} %bitcast.34) | data formatting | bytes 14680064
  147.3 1.3 broadcast_in_dim.31
  148.6 2.1 constant_dynamic-update-slice_fusion.2
  150.8 2.3 constant_dynamic-update-slice_fusion.1
  153.1 2.3 constant_dynamic-update-slice_fusion
  155.3 45.7 %collective-permute-done.3 = bf16[192,7168]{1,0:T(8,128)(2,1)} collective-permute-done((bf16[192,7168]{1,0:T(8,128)(2,1)}, bf16[192,7168]{1,0:T(8,128)(2,1)}, u32[]{:S(2)}, u32[]{:S(2)}) %collective-permute-start.3) | collective-permute-done | bytes 2752544 | tf_op jit(solution)/shard_map/ppermute | solution.py:16
  201.0 2.1 constant_dynamic-update-slice_fusion.3
  203.2 7.0 %fusion.13 = f32[768,512]{1,0:T(8,128)} fusion(bf16[768,7168]{1,0:T(8,128)(2,1)S(1)} %constant_dynamic-update-slice_fusion.3, bf16[7168,512]{1,0:T(8,128)(2,1)S(1)} %bitcast.37), kind=kOutput, calls=%fused_computation.37 | convolution fusion | flops 5637144576 | bytes 19922944 | tf_op jit(solution)/shard_map/dot_general | solution.py:35
  210.1 7.2 %convolution_convert_fusion = bf16[768,7168]{1,0:T(8,128)(2,1)} fusion(bf16[1,1,256,7168]{3,2,1,0:T(8,128)(2,1)S(1)} %copy-done, f32[768,512]{1,0:T(8,128)} %fusion.13), kind=kOutput, calls=%fused_computation.4 | convolution fusion | flops 2825256960 | bytes 16252928 | tf_op jit(solution)/shard_map/dot_general | solution.py:66
  217.4 102.1 %reduce-scatter.2.cloned.1.call-done = bf16[192,7168]{1,0:T(8,128)(2,1)} async-done(((bf16[768,7168]{1,0:T(8,128)(2,1)}), bf16[192,7168]{1,0:T(8,128)(2,1)}) %reduce-scatter.2.cloned.1.call-update) | async-done | bytes 2752528 | tf_op jit(solution)/shard_map/reduce_scatter | solution.py:65
  319.5 5.2 %all-to-all-start.1 = ((bf16[8,24,7168]{2,1,0:T(8,128)(2,1)}), bf16[8,24,7168]{2,1,0:T(8,128)(2,1)}, u32[]{:S(2)}, u32[]{:S(2)}) async-start(bf16[8,24,7168]{2,1,0:T(8,128)(2,1)} %bitcast.38), calls=%async_computation.2 | async-start | bytes 5505024 | tf_op jit(solution)/shard_map/all_to_all | solution.py:71
  324.8 33.2 %all-to-all-done.1 = bf16[8,24,7168]{2,1,0:T(8,128)(2,1)} async-done(((bf16[8,24,7168]{2,1,0:T(8,128)(2,1)}), bf16[8,24,7168]{2,1,0:T(8,128)(2,1)}, u32[]{:S(2)}, u32[]{:S(2)}) %all-to-all-start.1) | async-done | bytes 2752544 | tf_op jit(solution)/shard_map/all_to_all | solution.py:71
  358.0 5.5 %gather_fusion.1 = bf16[128,7168]{1,0:T(8,128)(2,1)S(1)} fusion(bf16[192,7168]{1,0:T(8,128)(2,1)} %bitcast.7, s32[1024]{0:T(1024)S(1)} %pad_clamp_fusion), kind=kCustom, calls=%fused_computation.1 | custom fusion | bytes 3670528 | tf_op jit(solution)/shard_map/gather | solution.py:78
  363.5 1.7 reshape.53
  365.2 3.5 fusion.14
  368.7 1.3 fusion.2
  (24 shorter events, 0.5 us)
Async XLA Ops:
  6.5 312.9 %reduce-scatter.2.cloned.1.call-start = ((), (), s32[]{:S(2)}) async-start(), calls=%async_computation.3 | async-start | bytes 13762560 | tf_op jit(solution)/shard_map/reduce_scatter | solution.py:65
  6.5 26.7 %collective-permute-start = (bf16[1,64,7168]{2,1,0:T(8,128)(2,1)}, bf16[1,64,7168]{2,1,0:T(8,128)(2,1)S(1)}, u32[]{:S(2)}, u32[]{:S(2)}) collective-permute-start(bf16[1,64,7168]{2,1,0:T(8,128)(2,1)} %param.5), channel_id=1, source_target_pairs={{0,32},{32,64},{64,96},{96,128},{128,160},{160,192},{192,224},{224... | collective-permute-start | bytes 2752520 | tf_op jit(solution)/shard_map/ppermute | solution.py:31
  78.1 61.9 %collective-permute-start.1 = (bf16[192,7168]{1,0:T(8,128)(2,1)}, bf16[192,7168]{1,0:T(8,128)(2,1)}, u32[]{:S(2)}, u32[]{:S(2)}) collective-permute-start(bf16[192,7168]{1,0:T(8,128)(2,1)} %bitcast.4), channel_id=1, source_target_pairs={{0,8},{8,16},{16,24},{24,0},{1,9},{9,17},{17,25},{25,1},{2,10},{10... | collective-permute-start | bytes 8257544 | tf_op jit(solution)/shard_map/ppermute | solution.py:16
  79.3 73.8 %collective-permute-start.2 = (bf16[192,7168]{1,0:T(8,128)(2,1)}, bf16[192,7168]{1,0:T(8,128)(2,1)}, u32[]{:S(2)}, u32[]{:S(2)}) collective-permute-start(bf16[192,7168]{1,0:T(8,128)(2,1)} %bitcast.4), channel_id=1, source_target_pairs={{0,24},{8,0},{16,8},{24,16},{1,25},{9,1},{17,9},{25,17},{2,26},{10... | collective-permute-start | bytes 8257544 | tf_op jit(solution)/shard_map/ppermute | solution.py:21
  140.0 61.0 %collective-permute-start.3 = (bf16[192,7168]{1,0:T(8,128)(2,1)}, bf16[192,7168]{1,0:T(8,128)(2,1)}, u32[]{:S(2)}, u32[]{:S(2)}) collective-permute-start(bf16[192,7168]{1,0:T(8,128)(2,1)} %collective-permute-done.1), channel_id=1, source_target_pairs={{0,8},{8,16},{16,24},{24,0},{1,9},{9,17},{17,25},{25,1},{2,10},{10... | collective-permute-start | bytes 8257544 | tf_op jit(solution)/shard_map/ppermute | solution.py:16
  150.8 52.3 %slice-start = ((s8[7340032]{0:T(1024)(128)(4,1)}), s8[4194304]{0:T(1024)(128)(4,1)S(1)}, s32[]{:S(2)}) async-start(s8[7340032]{0:T(1024)(128)(4,1)} %bitcast.35), calls=%async_computation.4 | async-start | bytes 8388608
  153.0 50.1 %slice-start.1 = ((s8[7340032]{0:T(1024)(128)(4,1)}), s8[3145728]{0:T(1024)(128)(4,1)S(1)}, s32[]{:S(2)}) async-start(s8[7340032]{0:T(1024)(128)(4,1)} %bitcast.35), calls=%async_computation.5 | async-start | bytes 6291456
  203.1 7.0 %copy-start = (bf16[1,1,256,7168]{3,2,1,0:T(8,128)(2,1)S(1)}, bf16[1,1,256,7168]{3,2,1,0:T(8,128)(2,1)}, u32[]{:S(2)}) copy-start(bf16[1,1,256,7168]{3,2,1,0:T(8,128)(2,1)} %param.9) | copy-start | bytes 11010052
  319.5 5.2 %copy-start.1 = (f32[1,64,2]{1,2,0:T(2,128)S(1)}, f32[1,64,2]{1,2,0:T(2,128)}, u32[]{:S(2)}) copy-start(f32[1,64,2]{1,2,0:T(2,128)} %param.7) | copy-start | bytes 1540
  319.5 38.5 %all-to-all-start.1 = ((bf16[8,24,7168]{2,1,0:T(8,128)(2,1)}), bf16[8,24,7168]{2,1,0:T(8,128)(2,1)}, u32[]{:S(2)}, u32[]{:S(2)}) async-start(bf16[8,24,7168]{2,1,0:T(8,128)(2,1)} %bitcast.38), calls=%async_computation.2 | async-start | bytes 5505024 | tf_op jit(solution)/shard_map/all_to_all | solution.py:71
Sparse Core Ops, SparseCore 0:
  217.5 101.9 reduce-scatter.1
